TPU v7x, 32 devices: a whole 2x2x4 slice. The times are simulated.
32 devices in a mesh: lat: 16 (over z, y, x), fld: 2 (over core).
Axes of the slice: x: 2, y: 2, z: 4, core: 2. Of those that a mesh axis runs over, the one named last changes fastest.
Arguments:
- grid: bfloat16 [2, 4, 69, 640, 1408], P('fld', None, None, 'lat'), may hold values from -6 to 6
- cycle_ids: int32 [640], replicated, may hold values from 0 to 639, each once
- cycle_len: int32 [640], replicated, may hold values from 20 to 1296, as said below
- wave_ids: int32 [320], replicated, may hold values from 0 to 319, each once
- legendre: bfloat16 [320, 320, 640], P('lat'), may hold values from -0.25 to 0.25
- target: float32 [2, 4, 69, 2, 320, 320], P('fld', None, None, None, 'lat'), may hold values from -18 to 18
- step_w: float32 [2], P('fld'), may hold values from 0.5 to 2
- chan_w: float32 [69], replicated, may hold values from 0.2 to 2
Outputs:
- coeffs: float32 [2, 4, 69, 2, 320, 320], P('fld', None, None, None, 'lat')
- loss: float32 [], replicated
- field_grad: bfloat16 [2, 4, 69, 640, 1408], P('fld', None, None, 'lat')
Inputs may be any that keep to these rules, and one draw needn't show every extreme that they name: `cycle_len`: every length 20 + 4 j with j from 0 to 319 occurs exactly twice.
All inputs are finite; a program needn't handle non-finite values.
Results may differ from a plain program's by a relative error of at most 0.0065.
Values may be sent and summed in bfloat16 or wider, within the bound.
No kernel may reach another device: no remote copies, remote signals or barrier semaphores. Data moves between devices by JAX's collectives and lax.ppermute only.
A program may use at most 320 MiB of HBM per device.

v0:
```python
import math
import jax
import jax.numpy as jnp
from jax import lax
from jax.sharding import PartitionSpec as P

STEPS = 2


def cycle_table(length, wave_order, segment):
    slot_index = jnp.arange(segment, dtype=jnp.int32)
    phase_int = slot_index[:, None] * wave_order[None, :] % length
    angles = 2.0 * math.pi / length.astype(jnp.float32) * phase_int.astype(jnp.float32)
    inside = (slot_index[:, None] < length) & (2 * wave_order[None, :] < length)
    row_scale = jnp.where(inside, lax.rsqrt(length.astype(jnp.float32)), jnp.float32(0.0))
    paired = jnp.stack([jnp.cos(angles) * row_scale, -jnp.sin(angles) * row_scale], axis=2)
    return paired.reshape(segment, 2 * wave_order.shape[0]).astype(jnp.bfloat16)


def owner_pass(
    part_fourier, legendre_cols, kept_mask, factor, target_part, weight_part, send_out, send_back
):
    gathered = send_out(part_fourier)
    coeffs = jnp.einsum(
        "jnr,rbjp->jnbp", legendre_cols, gathered, preferred_element_type=jnp.float32
    )
    coeffs = coeffs * kept_mask
    weight = factor[:, None, None, None] * weight_part[None, None, :, None]
    misfit = (coeffs - target_part) * kept_mask
    partial_value = jnp.sum(weight * misfit * misfit)
    grad_coeff = (2.0 * weight * misfit).astype(jnp.bfloat16)
    back_rows = jnp.einsum(
        "jnr,jnbp->rbjp", legendre_cols, grad_coeff, preferred_element_type=jnp.float32
    )
    back_rows = back_rows.astype(jnp.bfloat16)
    returned = send_back(back_rows)
    return (coeffs, partial_value, returned)


def per_device(grid, cycle_ids, cycle_len, wave_ids, legendre, target, step_w, chan_w):
    batch_size, chan_count, cycle_dev, segment = (
        grid.shape[1],
        grid.shape[2],
        grid.shape[3],
        grid.shape[4],
    )
    wave_count = wave_ids.shape[0]
    wave_dev = legendre.shape[0]
    col_count = batch_size * chan_count
    lat_index = lax.axis_index("lat")
    my_cycles = lax.dynamic_slice_in_dim(cycle_ids, lat_index * cycle_dev, cycle_dev)
    lengths = jnp.take(cycle_len, my_cycles)
    tables = jax.vmap(lambda length: cycle_table(length, wave_ids, segment))(lengths)
    fourier = jnp.einsum("bcrk,rkj->rbcj", grid[0], tables, preferred_element_type=jnp.float32)
    fourier = fourier.astype(jnp.bfloat16).reshape(cycle_dev, col_count, wave_count, 2)
    my_waves = lax.dynamic_slice_in_dim(wave_ids, lat_index * wave_dev, wave_dev)
    legendre_cols = jnp.take(legendre, cycle_ids, axis=2)
    degree = jnp.arange(wave_count, dtype=jnp.int32)
    kept_mask = (degree[None, :] >= my_waves[:, None]).astype(jnp.float32)[:, :, None, None]
    target_local = jnp.transpose(
        target[0].reshape(col_count, 2, wave_dev, wave_count), (2, 3, 0, 1)
    )
    factor = jnp.where(my_waves == 0, 1.0, 2.0).astype(jnp.float32)
    weight_cols = jnp.broadcast_to(step_w[0] * chan_w[None, :], (batch_size, chan_count)).reshape(
        col_count
    )

    def send_out(values):
        return lax.all_to_all(values, "lat", split_axis=2, concat_axis=0, tiled=True)

    def send_back(values):
        return lax.all_to_all(values, "lat", split_axis=0, concat_axis=2, tiled=True)

    coeff_piece, partial_piece, returned_piece = owner_pass(
        fourier, legendre_cols, kept_mask, factor, target_local, weight_cols, send_out, send_back
    )
    returned = returned_piece
    returned = returned.reshape(cycle_dev, col_count, 2 * wave_count)
    field_rows = jnp.einsum("rbj,rkj->brk", returned, tables, preferred_element_type=jnp.float32)
    field_grad = field_rows.astype(jnp.bfloat16).reshape(
        1, batch_size, chan_count, cycle_dev, segment
    )
    coeff_out = jnp.transpose(coeff_piece, (2, 3, 0, 1)).reshape(
        1, batch_size, chan_count, 2, wave_dev, wave_count
    )
    loss_sum = lax.psum(partial_piece, ("lat", "fld"))
    term_count = STEPS * batch_size * chan_count * wave_count * (wave_count + 1) // 2
    loss = loss_sum / jnp.float32(term_count)
    return (coeff_out, loss, field_grad)


def solution(mesh):
    return jax.shard_map(
        per_device,
        mesh=mesh,
        in_specs=(
            P("fld", None, None, "lat", None),
            P(),
            P(),
            P(),
            P("lat", None, None),
            P("fld", None, None, None, "lat", None),
            P("fld"),
            P(),
        ),
        out_specs=(P("fld", None, None, None, "lat", None), P(), P("fld", None, None, "lat", None)),
        check_vma=False,
    )
```

profile of v0, /device:TPU:0, one launch (start us, length us, event | category | flops | bytes accessed | tf_op | source)
XLA Modules:
  0.0 2604.8 jit_solution(16800594429964141860)
XLA Ops:
  0.6 0.0 copy-start
  0.7 0.8 compare_select_fusion.2
  1.4 0.0 copy-done
  1.4 0.7 gather_fusion.1
  2.2 0.8 broadcast_compare_fusion.1
  2.9 0.1 iota_compare_fusion
  3.1 0.7 broadcast_multiply_fusion.2
  3.7 0.9 iota_multiply_fusion
  4.6 0.1 broadcast_compare_fusion
  4.7 1187.4 %fusion = (bf16[40,1408,320,1]{1,0,3,2:T(8,128)(2,1)}, bf16[40,1408,320,1]{1,0,3,2:T(8,128)(2,1)}) fusion(f32[40]{0:T(128)S(1)} %get-tuple-element.17, s32[40]{0:T(128)S(1)} %compare_select_fusion.1, s32[1408,320]{0,1:T(8,128)S(1)} %iota_multiply_fusion, f32[40]{0:T(128)S(1)} %get-tuple-element.16, pred[40]{0:T(512)(128)(4,1)S(1)} %get-tuple-element.8, ...), kind=kLoop, calls=%fused_computation.8 | loop fusion | flops 288358400 | bytes 73961480 | tf_op jit(solution)/shard_map/convert
  1192.1 48.1 %pad_maximum_fusion = bf16[40,1408,320,2]{1,0,3,2:T(8,128)(2,1)} fusion(bf16[40,1408,320,1]{1,0,3,2:T(8,128)(2,1)} %get-tuple-element.13, bf16[40,1408,320,1]{1,0,3,2:T(8,128)(2,1)} %get-tuple-element.12), kind=kLoop, calls=%fused_computation.15 | loop fusion | flops 36044800 | bytes 144179200 | tf_op jit(solution)/shard_map/vmap()/stack | solution.py:16
  1240.2 88.0 %convert_bitcast_fusion.1 = bf16[40,4,69,640]{3,2,1,0:T(8,128)(2,1)} fusion(bf16[4,69,40,1408]{3,2,1,0:T(8,128)(2,1)} %bitcast.51, bf16[40,1408,640,1]{1,0,2,3:T(8,128)(2,1)} %bitcast.3), kind=kOutput, calls=%fused_computation.31 | convolution fusion | flops 19903795200 | bytes 117309440 | tf_op jit(solution)/shard_map/bcrk,rkj->rbcj/dot_general | solution.py:54
  1328.2 41.0 %copy.35 = bf16[40,4,69,640]{2,1,0,3:T(4,128)(2,1)} copy(bf16[40,4,69,640]{3,2,1,0:T(8,128)(2,1)} %convert_bitcast_fusion.1) | data formatting | bytes 28262400 | tf_op jit(solution)/shard_map/convert_element_type | solution.py:55
  1369.2 40.3 %reshape.263 = bf16[40,276,320,2]{1,0,3,2:T(8,128)(2,1)} reshape(bf16[40,4,69,640]{2,1,0,3:T(4,128)(2,1)} %copy.35) | data formatting | bytes 28262400 | tf_op jit(solution)/shard_map/reshape | solution.py:55
  1409.6 8.6 all-to-all-start
  1418.2 0.0 copy-start.3
  1418.2 15.0 copy.32
  1433.2 0.0 copy-done.3
  1433.2 25.5 gather_fusion
  1458.7 0.0 copy-start.4
  1458.7 11.0 select_bitcast_fusion
  1469.8 14.9 copy.49
  1485.3 0.0 copy-done.4
  1485.3 0.1 mul.164
  1485.4 0.8 compare_select_fusion.3
  1486.1 0.1 fusion.25
  1486.2 0.1 broadcast_multiply_fusion
  1486.3 300.9 %all-to-all-done = bf16[40,276,320,2]{1,0,3,2:T(8,128)(2,1)} async-done(((bf16[40,276,320,2]{1,0,3,2:T(8,128)(2,1)}), bf16[40,276,320,2]{1,0,3,2:T(8,128)(2,1)}, u32[]{:S(2)}, u32[]{:S(2)}) %all-to-all-start) | async-done | bytes 14131232 | tf_op jit(solution)/shard_map/all_to_all | solution.py:69
  1787.2 0.0 copy-start.2
  1787.2 17.2 copy.36
  1804.4 0.0 copy-done.2
  1804.4 18.7 fusion.26
  1823.1 23.4 convert_bitcast_fusion.2
  1846.5 47.3 %copy.42 = bf16[640,276,20,2]{1,3,2,0:T(2,128)(2,1)} copy(bf16[640,276,20,2]{0,1,3,2:T(8,128)(2,1)} %convert_bitcast_fusion.2) | data formatting | bytes 28262400 | tf_op jit(solution)/shard_map/convert_element_type | solution.py:35
  1893.7 86.3 %all-to-all-start.1 = ((bf16[640,276,20,2]{1,3,2,0:T(2,128)(2,1)}), bf16[640,276,20,2]{1,3,2,0:T(2,128)(2,1)}, u32[]{:S(2)}, u32[]{:S(2)}) async-start(bf16[640,276,20,2]{1,3,2,0:T(2,128)(2,1)} %copy.42), calls=%async_computation.1 | async-start | bytes 39321600 | tf_op jit(solution)/shard_map/all_to_all | solution.py:72
  1980.0 19.0 fusion.17
  1999.0 447.4 %psum.7 = f32[]{:T(128)} all-reduce(f32[]{:T(128)} %get-tuple-element.10), channel_id=1, replica_groups=mesh['lat'=16,'fld'=2] {'lat','fld'}, use_global_device_ids=true, to_apply=%region_1.2 | all-reduce | flops 1 | bytes 8 | tf_op jit(solution)/shard_map/psum | solution.py:86
  2446.4 30.0 %copy.39 = f32[276,2,20,320]{3,1,2,0:T(2,128)} copy(f32[276,2,20,320]{3,0,1,2:T(8,128)} %get-tuple-element.11) | data formatting | bytes 28262400 | tf_op jit(solution)/shard_map/mul | solution.py:27
  2477.0 0.0 all-to-all-done.1
  2477.0 11.8 copy.43
  2488.9 7.0 copy.44
  2495.9 0.0 copy-start.1
  2495.9 72.0 %convert_bitcast_fusion = bf16[276,40,1408]{2,0,1:T(8,128)(2,1)} fusion(bf16[40,1408,640]{1,0,2:T(8,128)(2,1)} %bitcast.2, bf16[40,276,640]{1,0,2:T(8,128)(2,1)} %bitcast.49), kind=kOutput, calls=%fused_computation.23 | convolution fusion | flops 19912273920 | bytes 117309440 | tf_op jit(solution)/shard_map/rbj,rkj->brk/dot_general | solution.py:79
  2567.9 35.6 %copy.47 = bf16[276,40,1408]{2,1,0:T(8,128)(2,1)} copy(bf16[276,40,1408]{2,0,1:T(8,128)(2,1)} %convert_bitcast_fusion) | data formatting | bytes 62177280 | tf_op jit(solution)/shard_map/convert_element_type | solution.py:80
  2603.5 0.0 copy-done.1
  (8 shorter events, 0.0 us)
Async XLA Ops:
  0.6 0.8 copy-start
  1409.6 377.6 %all-to-all-start = ((bf16[40,276,320,2]{1,0,3,2:T(8,128)(2,1)}), bf16[40,276,320,2]{1,0,3,2:T(8,128)(2,1)}, u32[]{:S(2)}, u32[]{:S(2)}) async-start(bf16[40,276,320,2]{1,0,3,2:T(8,128)(2,1)} %reshape.263), calls=%async_computation | async-start | bytes 39321600 | tf_op jit(solution)/shard_map/all_to_all | solution.py:69
  1418.2 15.0 copy-start.3
  1458.7 26.5 %copy-start.4 = (f32[69]{0:T(128)S(1)}, f32[69]{0:T(128)}, u32[]{:S(2)}) copy-start(f32[69]{0:T(128)} %param.15) | copy-start | bytes 832
  1787.2 17.2 copy-start.2
  1893.7 583.3 %all-to-all-start.1 = ((bf16[640,276,20,2]{1,3,2,0:T(2,128)(2,1)}), bf16[640,276,20,2]{1,3,2,0:T(2,128)(2,1)}, u32[]{:S(2)}, u32[]{:S(2)}) async-start(bf16[640,276,20,2]{1,3,2,0:T(2,128)(2,1)} %copy.42), calls=%async_computation.1 | async-start | bytes 39321600 | tf_op jit(solution)/shard_map/all_to_all | solution.py:72
  2495.9 107.6 %copy-start.1 = (s32[640]{0:T(1024)S(1)}, s32[640]{0:T(1024)}, u32[]{:S(2)}) copy-start(s32[640]{0:T(1024)} %param.10) | copy-start | bytes 7684
where the time goes:
time: 2610 us; the launch traced here: 2600 us
  other arithmetic  1270 us (49%)
  blocking collectives  447 us (17%)
  waiting for transfers between devices  301 us (12%)
  local copies, waits for them, and re-layouts  287 us (11%)
  matrix products  202 us (8%)
  starting transfers between devices  94.9 us (4%)
    another operation x1, other arithmetic  1190 us
    psum x1, blocking collectives, per_device(): loss_sum = lax.psum(partial_piece, ('lat', 'fld'))  447 us
    all_to_all x1, waiting for transfers between devices, send_out(): lax.all_to_all(values, 'lat', split_axis=2, concat_axis=0, tiled=True)  301 us
    dot_general x1, matrix products, per_device(): jnp.einsum('bcrk,rkj->rbcj', grid[0], tables, preferred_element_type=jnp....  88 us
    all_to_all x1, starting transfers between devices, send_back(): lax.all_to_all(values, 'lat', split_axis=0, concat_axis=2, tiled=True)  86.3 us
    dot_general x1, matrix products, per_device(): jnp.einsum('rbj,rkj->brk', returned, tables, preferred_element_type=jnp.f...  72 us
  transfers between devices with their start and end apart: 2, of which 1 were waited for; matrix products, arithmetic and copies ran while one was open for 4% of the time, Pallas kernels for 0%

commit v1 on v0

--- a/solution.py
+++ b/solution.py
@@ -83,7 +83,7 @@
     coeff_out = jnp.transpose(coeff_piece, (2, 3, 0, 1)).reshape(
         1, batch_size, chan_count, 2, wave_dev, wave_count
     )
-    loss_sum = lax.psum(partial_piece, ("lat", "fld"))
+    loss_sum = jnp.sum(lax.all_gather(partial_piece, ("lat", "fld")), axis=0)
     term_count = STEPS * batch_size * chan_count * wave_count * (wave_count + 1) // 2
     loss = loss_sum / jnp.float32(term_count)
     return (coeff_out, loss, field_grad)

time: 2610 us -> 2610 us (level)
    psum x1 -> x0, blocking collectives: 447 us -> none  [per_device(): loss_sum = lax.psum(partial_piece, ('lat', 'fld'))]
    unnamed x0 -> x1, blocking collectives: none -> 447 us
  transfers between devices with their start and end apart: 2 -> 2, of which waited for: 1 -> 1; matrix products, arithmetic and copies ran while one was open for 4% -> 5% of each run, Pallas kernels for 0% -> 0%
where the time goes in v1:
time: 2610 us
  other arithmetic  1270 us (49%)
  blocking collectives  447 us (17%)
  waiting for transfers between devices  301 us (12%)
  local copies, waits for them, and re-layouts  287 us (11%)
  matrix products  202 us (8%)
  starting transfers between devices  94.9 us (4%)
    another operation x1, other arithmetic  1190 us
    unnamed x1, blocking collectives  447 us
    all_to_all x1, waiting for transfers between devices, send_out(): lax.all_to_all(values, 'lat', split_axis=2, concat_axis=0, tiled=True)  301 us
    dot_general x1, matrix products, per_device(): jnp.einsum('bcrk,rkj->rbcj', grid[0], tables, preferred_element_type=jnp....  88 us
    all_to_all x1, starting transfers between devices, send_back(): lax.all_to_all(values, 'lat', split_axis=0, concat_axis=2, tiled=True)  86.3 us
    dot_general x1, matrix products, per_device(): jnp.einsum('rbj,rkj->brk', returned, tables, preferred_element_type=jnp.f...  72 us
  transfers between devices with their start and end apart: 2, of which 1 were waited for; matrix products, arithmetic and copies ran while one was open for 5% of the time, Pallas kernels for 0%

profile of v1, /device:TPU:0, one launch (start us, length us, event | category | flops | bytes accessed | tf_op | source)
XLA Modules:
  0.0 2605.4 jit_solution(344248687325156076)
XLA Ops:
  0.6 0.0 copy-start
  0.7 0.8 compare_select_fusion.2
  1.4 0.0 copy-done
  1.4 0.7 gather_fusion.1
  2.2 0.8 broadcast_compare_fusion.1
  2.9 0.1 iota_compare_fusion
  3.1 0.7 broadcast_multiply_fusion.2
  3.7 0.9 iota_multiply_fusion
  4.6 0.1 broadcast_compare_fusion
  4.7 1187.4 %fusion = (bf16[40,1408,320,1]{1,0,3,2:T(8,128)(2,1)}, bf16[40,1408,320,1]{1,0,3,2:T(8,128)(2,1)}) fusion(f32[40]{0:T(128)S(1)} %get-tuple-element.17, s32[40]{0:T(128)S(1)} %compare_select_fusion.1, s32[1408,320]{0,1:T(8,128)S(1)} %iota_multiply_fusion, f32[40]{0:T(128)S(1)} %get-tuple-element.16, pred[40]{0:T(512)(128)(4,1)S(1)} %get-tuple-element.8, ...), kind=kLoop, calls=%fused_computation.8 | loop fusion | flops 288358400 | bytes 73961480 | tf_op jit(solution)/shard_map/convert
  1192.1 48.0 %pad_maximum_fusion = bf16[40,1408,320,2]{1,0,3,2:T(8,128)(2,1)} fusion(bf16[40,1408,320,1]{1,0,3,2:T(8,128)(2,1)} %get-tuple-element.13, bf16[40,1408,320,1]{1,0,3,2:T(8,128)(2,1)} %get-tuple-element.12), kind=kLoop, calls=%fused_computation.15 | loop fusion | flops 36044800 | bytes 144179200 | tf_op jit(solution)/shard_map/vmap()/stack | solution.py:16
  1240.2 88.0 %convert_bitcast_fusion.1 = bf16[40,4,69,640]{3,2,1,0:T(8,128)(2,1)} fusion(bf16[4,69,40,1408]{3,2,1,0:T(8,128)(2,1)} %bitcast.52, bf16[40,1408,640,1]{1,0,2,3:T(8,128)(2,1)} %bitcast.3), kind=kOutput, calls=%fused_computation.31 | convolution fusion | flops 19903795200 | bytes 117309440 | tf_op jit(solution)/shard_map/bcrk,rkj->rbcj/dot_general | solution.py:54
  1328.2 41.0 %copy.35 = bf16[40,4,69,640]{2,1,0,3:T(4,128)(2,1)} copy(bf16[40,4,69,640]{3,2,1,0:T(8,128)(2,1)} %convert_bitcast_fusion.1) | data formatting | bytes 28262400 | tf_op jit(solution)/shard_map/convert_element_type | solution.py:55
  1369.2 40.3 %reshape.263 = bf16[40,276,320,2]{1,0,3,2:T(8,128)(2,1)} reshape(bf16[40,4,69,640]{2,1,0,3:T(4,128)(2,1)} %copy.35) | data formatting | bytes 28262400 | tf_op jit(solution)/shard_map/reshape | solution.py:55
  1409.5 8.6 all-to-all-start
  1418.1 0.0 copy-start.3
  1418.1 15.0 copy.32
  1433.1 0.0 copy-done.3
  1433.1 25.5 gather_fusion
  1458.7 0.0 copy-start.4
  1458.7 11.0 select_bitcast_fusion
  1469.7 14.9 copy.49
  1485.2 0.0 copy-done.4
  1485.3 0.1 mul.164
  1485.4 0.8 compare_select_fusion.3
  1486.1 0.1 fusion.25
  1486.2 0.1 broadcast_multiply_fusion
  1486.3 300.9 %all-to-all-done = bf16[40,276,320,2]{1,0,3,2:T(8,128)(2,1)} async-done(((bf16[40,276,320,2]{1,0,3,2:T(8,128)(2,1)}), bf16[40,276,320,2]{1,0,3,2:T(8,128)(2,1)}, u32[]{:S(2)}, u32[]{:S(2)}) %all-to-all-start) | async-done | bytes 14131232 | tf_op jit(solution)/shard_map/all_to_all | solution.py:69
  1787.1 0.0 copy-start.2
  1787.1 17.2 copy.36
  1804.4 0.0 copy-done.2
  1804.4 18.7 fusion.26
  1823.0 23.3 convert_bitcast_fusion.2
  1846.4 47.3 %copy.42 = bf16[640,276,20,2]{1,3,2,0:T(2,128)(2,1)} copy(bf16[640,276,20,2]{0,1,3,2:T(8,128)(2,1)} %convert_bitcast_fusion.2) | data formatting | bytes 28262400 | tf_op jit(solution)/shard_map/convert_element_type | solution.py:35
  1893.7 86.3 %all-to-all-start.1 = ((bf16[640,276,20,2]{1,3,2,0:T(2,128)(2,1)}), bf16[640,276,20,2]{1,3,2,0:T(2,128)(2,1)}, u32[]{:S(2)}, u32[]{:S(2)}) async-start(bf16[640,276,20,2]{1,3,2,0:T(2,128)(2,1)} %copy.42), calls=%async_computation.1 | async-start | bytes 39321600 | tf_op jit(solution)/shard_map/all_to_all | solution.py:72
  1980.0 18.9 fusion.17
  1998.9 0.8 dynamic-update-slice
  1999.7 446.6 %all-reduce = f32[32]{0:T(128)S(1)} all-reduce(f32[32]{0:T(128)S(1)} %dynamic-update-slice), channel_id=1, replica_groups=mesh['lat'=16,'fld'=2] {'lat','fld'}, use_global_device_ids=true, to_apply=%add | all-reduce | flops 32 | bytes 256
  2446.3 30.0 %copy.39 = f32[276,2,20,320]{3,1,2,0:T(2,128)} copy(f32[276,2,20,320]{3,0,1,2:T(8,128)} %get-tuple-element.11) | data formatting | bytes 28262400 | tf_op jit(solution)/shard_map/mul | solution.py:27
  2476.3 0.6 reduce_sum.19
  2477.6 0.0 all-to-all-done.1
  2477.6 11.8 copy.43
  2489.4 7.0 copy.44
  2496.5 0.0 copy-start.1
  2496.5 72.0 %convert_bitcast_fusion = bf16[276,40,1408]{2,0,1:T(8,128)(2,1)} fusion(bf16[40,1408,640]{1,0,2:T(8,128)(2,1)} %bitcast.2, bf16[40,276,640]{1,0,2:T(8,128)(2,1)} %bitcast.50), kind=kOutput, calls=%fused_computation.23 | convolution fusion | flops 19912273920 | bytes 117309440 | tf_op jit(solution)/shard_map/rbj,rkj->brk/dot_general | solution.py:79
  2568.4 35.6 %copy.47 = bf16[276,40,1408]{2,1,0:T(8,128)(2,1)} copy(bf16[276,40,1408]{2,0,1:T(8,128)(2,1)} %convert_bitcast_fusion) | data formatting | bytes 62177280 | tf_op jit(solution)/shard_map/convert_element_type | solution.py:80
  2604.1 0.0 copy-done.1
  (9 shorter events, 0.0 us)
Async XLA Ops:
  0.6 0.8 copy-start
  1409.5 377.6 %all-to-all-start = ((bf16[40,276,320,2]{1,0,3,2:T(8,128)(2,1)}), bf16[40,276,320,2]{1,0,3,2:T(8,128)(2,1)}, u32[]{:S(2)}, u32[]{:S(2)}) async-start(bf16[40,276,320,2]{1,0,3,2:T(8,128)(2,1)} %reshape.263), calls=%async_computation | async-start | bytes 39321600 | tf_op jit(solution)/shard_map/all_to_all | solution.py:69
  1418.1 15.0 copy-start.3
  1458.7 26.6 %copy-start.4 = (f32[69]{0:T(128)S(1)}, f32[69]{0:T(128)}, u32[]{:S(2)}) copy-start(f32[69]{0:T(128)} %param.15) | copy-start | bytes 832
  1787.1 17.2 copy-start.2
  1893.7 583.9 %all-to-all-start.1 = ((bf16[640,276,20,2]{1,3,2,0:T(2,128)(2,1)}), bf16[640,276,20,2]{1,3,2,0:T(2,128)(2,1)}, u32[]{:S(2)}, u32[]{:S(2)}) async-start(bf16[640,276,20,2]{1,3,2,0:T(2,128)(2,1)} %copy.42), calls=%async_computation.1 | async-start | bytes 39321600 | tf_op jit(solution)/shard_map/all_to_all | solution.py:72
  2496.5 107.6 %copy-start.1 = (s32[640]{0:T(1024)S(1)}, s32[640]{0:T(1024)}, u32[]{:S(2)}) copy-start(s32[640]{0:T(1024)} %param.10) | copy-start | bytes 7684
